TPU v7x, 256 devices: a whole 4x4x8 slice. The times are simulated.
256 devices in a mesh: dp: 2 (over x_lo), expert: 128 (over y, z, x_hi, core).
Axes of the slice: x: 4 (x_hi: 2, x_lo: 2; x = x_hi * 2 + x_lo), y: 4, z: 8, core: 2. Of those that a mesh axis runs over, the one named last changes fastest.
Arguments:
- tokens: bfloat16 [256, 256, 1280], P(('dp', 'expert')), may hold values from -12 to 12
- router: bfloat16 [1280, 128], replicated, may hold values from -3 to 3
- w_in: bfloat16 [128, 1280, 5120], P('expert', None, 'dp'), may hold values from -0.15625 to 0.15625
- b_in: bfloat16 [128, 5120], P('expert'), may hold values from -3 to 3
- w_out: bfloat16 [128, 5120, 1280], P('expert', 'dp'), may hold values from -0.078125 to 0.078125
- b_out: bfloat16 [128, 1280], P('expert'), may hold values from -3 to 3
Outputs:
- mixed: bfloat16 [256, 256, 1280], P(('dp', 'expert'))
All inputs are finite; a program needn't handle non-finite values.
Results may differ from a plain program's by a relative error of at most 0.014.
Values may be sent and summed in bfloat16 or wider, within the bound.
A program may use at most 64 MiB of HBM per device.

v0:
```python
import functools

import jax
import jax.numpy as jnp
from jax import lax
from jax.experimental import pallas as pl
from jax.experimental.pallas import tpu as pltpu
from jax.sharding import PartitionSpec as P

MESH = pl.DeviceIdType.MESH
LANES = 128
SUBLANES = 16


def gelu(v):
    return v * (1.0 + lax.erf(v * (0.5**0.5))) * 0.5


def visit(n_dp, n_ex, me_dp, me_ex, action):
    half = n_ex // 2
    side = me_ex // half
    inner = lax.rem(me_ex, half)
    mirror = half - 1 - inner
    crossing = (1 - side) * half
    home = side * half

    def run(count, step):
        if count <= 8:
            for j in range(count):
                step(j)
        else:
            lax.fori_loop(0, count, lambda j, carry: step(j) or carry, 0)

    def far(j):
        for a in range(n_dp - 1, -1, -1):
            action(lax.rem(me_dp + a, n_dp), crossing + lax.rem(mirror - j + half, half))

    def near(j):
        for a in range(n_dp - 1, -1, -1):
            action(lax.rem(me_dp + a, n_dp), home + lax.rem(inner + 1 + j, half))

    run(half, far)
    run(half - 1, near)
    for a in range(n_dp - 1, 0, -1):
        action(lax.rem(me_dp + a, n_dp), me_ex)


def exchange(n_dp, n_ex, me_dp, me_ex, source, row_of, landing, send_sem, recv_sem, chunks):
    me = me_dp * n_ex + me_ex

    def send(a, e):
        pltpu.make_async_remote_copy(
            src_ref=source.at[row_of(a, e), pl.ds(0, chunks)],
            dst_ref=landing.at[me, pl.ds(0, chunks)],
            send_sem=send_sem,
            recv_sem=recv_sem,
            device_id=(a, e),
            device_id_type=MESH,
        ).start()

    visit(n_dp, n_ex, me_dp, me_ex, send)
    landing[me] = source[row_of(me_dp, me_ex)]


def wait_bytes(buffer, count, chunks, sem):
    rows = buffer.at[pl.ds(0, count), pl.ds(0, chunks)]
    pltpu.make_async_copy(rows, rows, sem).wait()


def kernel(
    n_dp,
    n_ex,
    tokens_hbm,
    router_hbm,
    w_in_hbm,
    b_in_hbm,
    w_out_hbm,
    b_out_hbm,
    comb_ref,
    eo,
    tok,
    router,
    w_in,
    b_in,
    w_out,
    b_out,
    wide_slots,
    wide_rows,
    send1,
    recv1,
    send2,
    recv2,
    x_ref,
    hid,
    load_sems,
    w_in_sems,
    w_out_sems,
    send_sems,
    recv_sems,
):
    n = n_dp * n_ex
    me_dp = lax.axis_index("dp")
    me_ex = lax.axis_index("expert")
    width = tok.shape[1]
    chunks = width // LANES
    pitch = send1.shape[1]

    loads = [
        pltpu.make_async_copy(tokens_hbm.at[0], tok, load_sems.at[0]),
        pltpu.make_async_copy(router_hbm, router, load_sems.at[1]),
        pltpu.make_async_copy(b_in_hbm, b_in, load_sems.at[2]),
        pltpu.make_async_copy(b_out_hbm, b_out, load_sems.at[3]),
    ]
    loads[0].start()
    loads[1].start()
    barrier = pltpu.get_barrier_semaphore()

    def greet(a, e):
        pl.semaphore_signal(barrier, inc=1, device_id=(a, e), device_id_type=MESH)

    visit(n_dp, n_ex, me_dp, me_ex, greet)

    def pieces(hbm, vmem, sems):
        count = sems.shape[0]
        rows = vmem.shape[0] // count
        return [
            pltpu.make_async_copy(
                hbm.at[0, pl.ds(i * rows, rows)], vmem.at[pl.ds(i * rows, rows)], sems.at[i]
            )
            for i in range(count)
        ]

    w_in_loads = pieces(w_in_hbm, w_in, w_in_sems)
    w_out_loads = pieces(w_out_hbm, w_out, w_out_sems)
    for load in w_in_loads + loads[2:] + w_out_loads:
        load.start()

    loads[0].wait()
    loads[1].wait()
    logits = lax.dot_general(
        router[...], tok[...], (((1,), (1,)), ((), ())), preferred_element_type=jnp.float32
    )
    over_tokens = jnp.exp(logits - jnp.max(logits, axis=1, keepdims=True))
    dispatch = (over_tokens / jnp.sum(over_tokens, axis=1, keepdims=True)).astype(jnp.bfloat16)
    slots = jnp.dot(dispatch, tok[...], preferred_element_type=jnp.float32)
    for j in range(chunks):
        wide_slots[pl.ds(j, n_ex, stride=pitch), :] = slots[:, j * LANES : (j + 1) * LANES]
    send1[...] = wide_slots[...].reshape(send1.shape).astype(jnp.bfloat16)

    pl.semaphore_wait(barrier, n - 1)
    exchange(
        n_dp, n_ex, me_dp, me_ex, send1, lambda a, e: e, recv1, send_sems.at[0], recv_sems.at[0], chunks
    )

    over_experts = jnp.exp(logits - jnp.max(logits, axis=0, keepdims=True))
    combine = over_experts / jnp.sum(over_experts, axis=0, keepdims=True)
    comb_ref[...] = combine.T.astype(jnp.bfloat16)

    for load in loads[2:] + w_in_loads:
        load.wait()
    wait_bytes(recv1, n - 1, chunks, recv_sems.at[0])
    wide_rows[...] = recv1[...].astype(jnp.float32).reshape(wide_rows.shape)
    for j in range(chunks):
        x_ref[:, j * LANES : (j + 1) * LANES] = wide_rows[pl.ds(j, n, stride=pitch), :].astype(jnp.bfloat16)

    half = w_in.shape[1]
    tile = 2 * LANES

    for at in range(0, half, tile):
        bias = b_in[:, pl.ds(pl.multiple_of(me_dp * half + at, LANES), tile)].astype(jnp.float32)
        v = jnp.dot(x_ref[...], w_in[:, at : at + tile], preferred_element_type=jnp.float32) + bias
        hid[:, at : at + tile] = gelu(v).astype(jnp.bfloat16)

    for load in w_out_loads:
        load.wait()
    keep = (me_dp == 0).astype(jnp.float32)
    for at in range(0, width, tile):
        y = jnp.dot(hid[...], w_out[:, at : at + tile], preferred_element_type=jnp.float32)
        y = y + keep * b_out[:, at : at + tile].astype(jnp.float32)
        for c in range(tile // LANES):
            wide_rows[pl.ds(at // LANES + c, n, stride=pitch), :] = y[:, c * LANES : (c + 1) * LANES]
    send2[...] = wide_rows[...].reshape(send2.shape).astype(jnp.bfloat16)

    exchange(
        n_dp, n_ex, me_dp, me_ex, send2, lambda a, e: a * n_ex + e, recv2, send_sems.at[1], recv_sems.at[1], chunks
    )
    wait_bytes(recv2, n - 1, chunks, recv_sems.at[1])
    wide_rows[...] = recv2[...].astype(jnp.float32).reshape(wide_rows.shape)
    for j in range(chunks):
        total = wide_rows[pl.ds(j, n_ex, stride=pitch), :]
        for a in range(1, n_dp):
            total = total + wide_rows[pl.ds(a * n_ex * pitch + j, n_ex, stride=pitch), :]
        eo[:, j * LANES : (j + 1) * LANES] = total.astype(jnp.bfloat16)
    wait_bytes(recv1, n - 1, chunks, send_sems.at[0])
    wait_bytes(recv2, n - 1, chunks, send_sems.at[1])


def mix_kernel(combine, expert_out, out_hbm, mixed, sems):
    count = sems.shape[0]
    tile = mixed.shape[1] // count
    writes = []
    for i in range(count):
        columns = pl.ds(i * tile, tile)
        mixed[:, columns] = jnp.dot(
            combine[...], expert_out[:, columns], preferred_element_type=jnp.float32
        ).astype(mixed.dtype)
        write = pltpu.make_async_copy(mixed.at[:, columns], out_hbm.at[0, :, columns], sems.at[i])
        write.start()
        writes.append(write)
    for write in writes:
        write.wait()


def shards(n_dp, n_ex, tokens, router, w_in, b_in, w_out, b_out):
    n = n_dp * n_ex
    images, m, width = tokens.shape
    assert images == 1 and w_in.shape[0] == 1
    half = w_in.shape[2]
    chunks = width // LANES
    pitch = -(-chunks // SUBLANES) * SUBLANES
    bf16, f32 = jnp.bfloat16, jnp.float32
    combine, expert_out = pl.pallas_call(
        functools.partial(kernel, n_dp, n_ex),
        out_shape=[
            pltpu.VMEM((m, n_ex), bf16),
            pltpu.VMEM((n_ex, width), bf16),
        ],
        in_specs=[pl.BlockSpec(memory_space=pltpu.HBM)] * 6,
        out_specs=[pl.BlockSpec(memory_space=pltpu.VMEM)] * 2,
        scratch_shapes=[
            pltpu.VMEM((m, width), bf16),
            pltpu.VMEM(router.shape[::-1], bf16),
            pltpu.VMEM(w_in.shape[1:], bf16),
            pltpu.VMEM(b_in.shape, bf16),
            pltpu.VMEM(w_out.shape[1:], bf16),
            pltpu.VMEM(b_out.shape, bf16),
            pltpu.VMEM((n_ex * pitch, LANES), f32),
            pltpu.VMEM((n * pitch, LANES), f32),
            pltpu.VMEM((n_ex, pitch, LANES), bf16),
            pltpu.VMEM((n, pitch, LANES), bf16),
            pltpu.VMEM((n, pitch, LANES), bf16),
            pltpu.VMEM((n, pitch, LANES), bf16),
            pltpu.VMEM((n, width), bf16),
            pltpu.VMEM((n, half), bf16),
            pltpu.SemaphoreType.DMA((4,)),
            pltpu.SemaphoreType.DMA((4,)),
            pltpu.SemaphoreType.DMA((4,)),
            pltpu.SemaphoreType.DMA((2,)),
            pltpu.SemaphoreType.DMA((2,)),
        ],
        compiler_params=pltpu.CompilerParams(
            collective_id=0, has_side_effects=True, vmem_limit_bytes=60 * 1024 * 1024
        ),
    )(tokens, router.T, w_in, b_in, w_out, b_out)
    tile = 2 * LANES
    return pl.pallas_call(
        mix_kernel,
        out_shape=jax.ShapeDtypeStruct(tokens.shape, bf16),
        in_specs=[pl.BlockSpec(memory_space=pltpu.VMEM)] * 2,
        out_specs=pl.BlockSpec(memory_space=pltpu.HBM),
        scratch_shapes=[
            pltpu.VMEM((m, width), bf16),
            pltpu.SemaphoreType.DMA((width // tile,)),
        ],
        compiler_params=pltpu.CompilerParams(vmem_limit_bytes=8 * 1024 * 1024),
    )(combine, expert_out)


def solution(mesh):
    return jax.shard_map(
        functools.partial(shards, mesh.shape["dp"], mesh.shape["expert"]),
        mesh=mesh,
        in_specs=(
            P(("dp", "expert"), None, None),
            P(),
            P("expert", None, "dp"),
            P("expert", None),
            P("expert", "dp", None),
            P("expert", None),
        ),
        out_specs=P(("dp", "expert"), None, None),
        check_vma=False,
    )
```

profile of v0, /device:TPU:1, one launch (start us, length us, event | category | flops | bytes accessed | tf_op | source)
XLA Modules:
  0.0 60.7 jit_solution(12616012906458037746)
XLA Ops:
  0.0 1.9 %copy.7 = bf16[1280,128]{0,1:T(8,128)(2,1)} copy(bf16[1280,128]{1,0:T(8,128)(2,1)} %param.7) | data formatting | bytes 655360 | tf_op args[1]
  1.9 57.8 %shard_map.64 = (bf16[256,128]{1,0:T(8,128)(2,1)S(1)}, bf16[128,1280]{1,0:T(8,128)(2,1)S(1)}) custom-call(bf16[1,256,1280]{2,1,0:T(8,128)(2,1)} %tokens_hbm.1, bf16[128,1280]{1,0:T(8,128)(2,1)} %bitcast.1, bf16[1,1280,2560]{2,1,0:T(8,128)(2,1)} %w_in_hbm.1, bf16[1,5120]{1,0:T(2,128)(2,1)} %b_in_hbm.1, bf16[1,2560,1280]{2,1,0:T(8,128)(2,1)} %w_out_hbm.1, ...), custom_call_target="tpu_custom_call" | custom-call | tf_op jit(solution)/shard_map/pallas_call | solution.py:222
  59.7 1.1 %shard_map.65 = bf16[1,256,1280]{2,1,0:T(8,128)(2,1)} custom-call(bf16[256,128]{1,0:T(8,128)(2,1)S(1)} %get-tuple-element.7.combine, bf16[128,1280]{1,0:T(8,128)(2,1)S(1)} %get-tuple-element.8.expert_out), custom_call_target="tpu_custom_call" | custom-call | tf_op jit(solution)/shard_map/pallas_call | solution.py:256
where the time goes:
time: 60.9 us; the launch traced here: 60.7 us
  Pallas kernels  58.9 us (97%)
  local copies, waits for them, and re-layouts  1.87 us (3%)
    pallas_call x1, Pallas kernels, shards(): pl.pallas_call(functools.partial(kernel, n_dp, n_ex), out_shape=[pltpu.VM...  57.8 us
    unnamed x1, local copies, waits for them, and re-layouts  1.87 us

commit v1 on v0

v1 whole, which is shorter than its diff:
```python
import functools

import jax
import jax.numpy as jnp
from jax import lax
from jax.experimental import pallas as pl
from jax.experimental.pallas import tpu as pltpu
from jax.sharding import PartitionSpec as P

MESH = pl.DeviceIdType.MESH
LANES = 128
PITCH = 16
NY, NZ, QUAD = 4, 8, 4
NQ = NY * QUAD
NP = 2 * NQ
SENDS_ORDER = (4, 3, 5, 2, 6, 1, 7)
FORWARD_ORDER = (0, 4, 3, 5, 2, 6, 1, 7)
REDUCE_ORDER = (4, 3, 5, 2, 6, 1, 7, 0)


def gelu(v):
    return v * (1.0 + lax.erf(v * (0.5**0.5))) * 0.5


def wait_copy(ref, sem):
    pltpu.make_async_copy(ref, ref, sem).wait()


def kernel(
    tokens_hbm,
    router_hbm,
    w_in_hbm,
    b_in_hbm,
    w_out_hbm,
    b_out_hbm,
    comb_ref,
    eo,
    tok,
    router,
    w_in,
    b_in,
    w_out,
    b_out,
    permuted,
    send1,
    zland,
    wide16,
    fwd,
    recv1,
    wide32,
    x_ref,
    hid,
    wide_rows,
    send2,
    recv2,
    total,
    eland,
    load_sems,
    w_in_sems,
    w_out_sems,
    send_sems,
    z_sems,
    plane1_sems,
    plane2_sems,
    eo_sem,
):
    me_dp = lax.axis_index("dp")
    me_ex = lax.axis_index("expert")
    me_y = me_ex // (NZ * QUAD)
    me_z = lax.rem(me_ex // QUAD, NZ)
    me_quad = lax.rem(me_ex, QUAD)
    me_xh, me_core = me_quad // 2, lax.rem(me_quad, 2)
    me_q = me_y * QUAD + me_quad
    me_p = me_dp * NQ + me_q
    width = tok.shape[1]
    chunks = width // LANES

    def along_z(d):
        z = lax.rem(me_z + d, NZ)
        return z, (me_dp, me_y * (NZ * QUAD) + z * QUAD + me_quad)

    ys = [lax.rem(me_y + dy, NY) for dy in range(NY)]
    quads = [lax.rem(me_xh + dx, 2) * 2 + lax.rem(me_core + dc, 2) for dc in range(2) for dx in range(2)]
    dps = [me_dp, 1 - me_dp]
    plane = []
    for t in range(NP - 1, 0, -1):
        y, a, quad = ys[t % NY], dps[t // NY % 2], quads[t // (2 * NY)]
        plane.append((a, y * QUAD + quad, (a, y * (NZ * QUAD) + me_z * QUAD + quad)))

    def each_in_plane(action):
        for target in plane:
            action(*target)

    def remote(src, dst, send_sem, recv_sem, device):
        pltpu.make_async_remote_copy(
            src_ref=src,
            dst_ref=dst,
            send_sem=send_sem,
            recv_sem=recv_sem,
            device_id=device,
            device_id_type=MESH,
        ).start()

    loads = [
        pltpu.make_async_copy(tokens_hbm.at[0], tok, load_sems.at[0]),
        pltpu.make_async_copy(router_hbm, router, load_sems.at[1]),
        pltpu.make_async_copy(b_in_hbm, b_in, load_sems.at[2]),
        pltpu.make_async_copy(b_out_hbm, b_out, load_sems.at[3]),
    ]
    loads[0].start()
    loads[1].start()
    barrier = pltpu.get_barrier_semaphore()

    def greet(device):
        pl.semaphore_signal(barrier, inc=1, device_id=device, device_id_type=MESH)

    with jax.named_scope("greet"):
        for d in SENDS_ORDER:
            greet(along_z(d)[1])
        each_in_plane(lambda a, q, device: greet(device))

    def pieces(hbm, vmem, sems):
        count = sems.shape[0]
        rows = vmem.shape[0] // count
        return [
            pltpu.make_async_copy(
                hbm.at[0, pl.ds(i * rows, rows)], vmem.at[pl.ds(i * rows, rows)], sems.at[i]
            )
            for i in range(count)
        ]

    w_in_loads = pieces(w_in_hbm, w_in, w_in_sems)
    w_out_loads = pieces(w_out_hbm, w_out, w_out_sems)
    for load in w_in_loads + loads[2:] + w_out_loads:
        load.start()

    with jax.named_scope("waittok"):
        loads[0].wait()
        loads[1].wait()
    with jax.named_scope("dispatch"):
        logits = jnp.dot(tok[...], router[...], preferred_element_type=jnp.float32).T
        for y in range(NY):
            for z in range(NZ):
                at = (y * NZ + z) * QUAD
                permuted[z * NQ + y * QUAD : z * NQ + (y + 1) * QUAD, :] = logits[at : at + QUAD, :]
        logits = permuted[...]
        over_tokens = jnp.exp(logits - jnp.max(logits, axis=1, keepdims=True))
        dispatch = (over_tokens / jnp.sum(over_tokens, axis=1, keepdims=True)).astype(jnp.bfloat16)
        send1[...] = jnp.dot(dispatch, tok[...], preferred_element_type=jnp.float32).astype(jnp.bfloat16)

    with jax.named_scope("barwait"):
        pl.semaphore_wait(barrier, NZ - 1 + NP - 1)

    with jax.named_scope("sendz"):
        for d in SENDS_ORDER:
            z, device = along_z(d)
            back = NZ - d
            remote(
                send1.at[pl.ds(pl.multiple_of(z * NQ, NQ), NQ)],
                zland.at[back],
                send_sems.at[0],
                z_sems.at[back],
                device,
            )

    def forward(r):
        if r == 0:
            block = send1[pl.ds(pl.multiple_of(me_z * NQ, NQ), NQ), :]
        else:
            wait_copy(zland.at[r], z_sems.at[r])
            block = zland[r]
        for j in range(chunks):
            wide16[r, pl.ds(j, NQ, stride=PITCH), :] = block[:, j * LANES : (j + 1) * LANES].astype(jnp.float32)
        fwd[r] = wide16[r].reshape(NQ, PITCH, LANES).astype(jnp.bfloat16)

        def send(a, q, device):
            remote(
                fwd.at[r, q, pl.ds(0, chunks)],
                recv1.at[r, me_p, pl.ds(0, chunks)],
                send_sems.at[1],
                plane1_sems.at[r],
                device,
            )

        each_in_plane(send)
        recv1[r, me_p] = fwd[r, me_q]

    with jax.named_scope("combine"):
        over_experts = jnp.exp(logits - jnp.max(logits, axis=0, keepdims=True))
        combine = over_experts / jnp.sum(over_experts, axis=0, keepdims=True)
        comb_ref[...] = combine.T.astype(jnp.bfloat16)

    for r in FORWARD_ORDER:
        with jax.named_scope("forward%d" % r):
            forward(r)

    for r in FORWARD_ORDER:
        with jax.named_scope("recv1_%d" % r):
            wait_copy(recv1.at[r, pl.ds(0, NP - 1), pl.ds(0, chunks)], plane1_sems.at[r])
            wide32[...] = recv1[r].astype(jnp.float32).reshape(wide32.shape)
            for j in range(chunks):
                x_ref[r * NP : (r + 1) * NP, j * LANES : (j + 1) * LANES] = wide32[
                    pl.ds(j, NP, stride=PITCH), :
                ].astype(jnp.bfloat16)

    for load in loads[2:] + w_in_loads:
        load.wait()
    half = w_in.shape[1]
    tile = 2 * LANES

    with jax.named_scope("mlp1"):
        for at in range(0, half, tile):
            bias = b_in[:, pl.ds(pl.multiple_of(me_dp * half + at, LANES), tile)].astype(jnp.float32)
            v = jnp.dot(x_ref[...], w_in[:, at : at + tile], preferred_element_type=jnp.float32) + bias
            hid[:, at : at + tile] = gelu(v).astype(jnp.bfloat16)

    for load in w_out_loads:
        load.wait()
    keep = (me_dp == 0).astype(jnp.float32)
    n = NZ * NP
    with jax.named_scope("mlp2"):
        for at in range(0, width, tile):
            y = jnp.dot(hid[...], w_out[:, at : at + tile], preferred_element_type=jnp.float32)
            y = y + keep * b_out[:, at : at + tile].astype(jnp.float32)
            for c in range(tile // LANES):
                wide_rows[pl.ds(at // LANES + c, n, stride=PITCH), :] = y[:, c * LANES : (c + 1) * LANES]
        send2[...] = wide_rows[...].reshape(send2.shape).astype(jnp.bfloat16)

    def scatter(r):
        def send(a, q, device):
            remote(
                send2.at[r, a * NQ + q, pl.ds(0, chunks)],
                recv2.at[r, me_p, pl.ds(0, chunks)],
                send_sems.at[2],
                plane2_sems.at[r],
                device,
            )

        each_in_plane(send)
        recv2[r, me_p] = send2[r, me_p]

    with jax.named_scope("scatter"):
        for r in REDUCE_ORDER:
            scatter(r)

    for r in REDUCE_ORDER:
        with jax.named_scope("reduce%d" % r):
            wait_copy(recv2.at[r, pl.ds(0, NP - 1), pl.ds(0, chunks)], plane2_sems.at[r])
            pair = recv2[r, :NQ].astype(jnp.float32) + recv2[r, NQ:].astype(jnp.float32)
            wide16[r] = pair.reshape(NQ * PITCH, LANES)
            for j in range(chunks):
                total[r, :, j * LANES : (j + 1) * LANES] = wide16[r, pl.ds(j, NQ, stride=PITCH), :].astype(jnp.bfloat16)
            mine = pl.ds(pl.multiple_of(me_z * NQ, NQ), NQ)
            if r == 0:
                eland[mine, :] = total[r]
            else:
                remote(total.at[r], eland.at[mine], send_sems.at[3], eo_sem, along_z(r)[1])

    with jax.named_scope("recv2"):
        wait_copy(eland.at[pl.ds(0, (NZ - 1) * NQ)], eo_sem)
    with jax.named_scope("tail"):
        eo[...] = eland[...]
        rows = recv1.at[:, pl.ds(0, NP - 1), pl.ds(0, chunks)]
        wait_copy(zland.at[pl.ds(0, NZ - 1)], send_sems.at[0])
        wait_copy(rows, send_sems.at[1])
        wait_copy(rows, send_sems.at[2])
        wait_copy(zland.at[pl.ds(0, NZ - 1)], send_sems.at[3])


def mix_kernel(combine, expert_out, out_hbm, mixed, sems):
    count = sems.shape[0]
    tile = mixed.shape[1] // count
    writes = []
    for i in range(count):
        columns = pl.ds(i * tile, tile)
        mixed[:, columns] = jnp.dot(
            combine[...], expert_out[:, columns], preferred_element_type=jnp.float32
        ).astype(mixed.dtype)
        write = pltpu.make_async_copy(mixed.at[:, columns], out_hbm.at[0, :, columns], sems.at[i])
        write.start()
        writes.append(write)
    for write in writes:
        write.wait()


def shards(tokens, router, w_in, b_in, w_out, b_out):
    images, m, width = tokens.shape
    n_ex = NZ * NQ
    n = NZ * NP
    assert images == 1 and w_in.shape[0] == 1 and router.shape[1] == n_ex
    half = w_in.shape[2]
    bf16, f32 = jnp.bfloat16, jnp.float32
    dma = pltpu.SemaphoreType.DMA
    combine, expert_out = pl.pallas_call(
        kernel,
        out_shape=[
            pltpu.VMEM((m, n_ex), bf16),
            pltpu.VMEM((n_ex, width), bf16),
        ],
        in_specs=[pl.BlockSpec(memory_space=pltpu.HBM)] * 6,
        out_specs=[pl.BlockSpec(memory_space=pltpu.VMEM)] * 2,
        scratch_shapes=[
            pltpu.VMEM((m, width), bf16),
            pltpu.VMEM(router.shape, bf16),
            pltpu.VMEM(w_in.shape[1:], bf16),
            pltpu.VMEM(b_in.shape, bf16),
            pltpu.VMEM(w_out.shape[1:], bf16),
            pltpu.VMEM(b_out.shape, bf16),
            pltpu.VMEM((n_ex, m), f32),
            pltpu.VMEM((n_ex, width), bf16),
            pltpu.VMEM((NZ, NQ, width), bf16),
            pltpu.VMEM((NZ, NQ * PITCH, LANES), f32),
            pltpu.VMEM((NZ, NQ, PITCH, LANES), bf16),
            pltpu.VMEM((NZ, NP, PITCH, LANES), bf16),
            pltpu.VMEM((NP * PITCH, LANES), f32),
            pltpu.VMEM((n, width), bf16),
            pltpu.VMEM((n, half), bf16),
            pltpu.VMEM((n * PITCH, LANES), f32),
            pltpu.VMEM((NZ, NP, PITCH, LANES), bf16),
            pltpu.VMEM((NZ, NP, PITCH, LANES), bf16),
            pltpu.VMEM((NZ, NQ, width), bf16),
            pltpu.VMEM((n_ex, width), bf16),
            dma((4,)),
            dma((4,)),
            dma((4,)),
            dma((4,)),
            dma((NZ,)),
            dma((NZ,)),
            dma((NZ,)),
            dma,
        ],
        compiler_params=pltpu.CompilerParams(
            collective_id=0, has_side_effects=True, vmem_limit_bytes=60 * 1024 * 1024
        ),
    )(tokens, router, w_in, b_in, w_out, b_out)
    tile = 2 * LANES
    return pl.pallas_call(
        mix_kernel,
        out_shape=jax.ShapeDtypeStruct(tokens.shape, bf16),
        in_specs=[pl.BlockSpec(memory_space=pltpu.VMEM)] * 2,
        out_specs=pl.BlockSpec(memory_space=pltpu.HBM),
        scratch_shapes=[
            pltpu.VMEM((m, width), bf16),
            dma((width // tile,)),
        ],
        compiler_params=pltpu.CompilerParams(vmem_limit_bytes=8 * 1024 * 1024),
    )(combine, expert_out)


def solution(mesh):
    return jax.shard_map(
        shards,
        mesh=mesh,
        in_specs=(
            P(("dp", "expert"), None, None),
            P(),
            P("expert", None, "dp"),
            P("expert", None),
            P("expert", "dp", None),
            P("expert", None),
        ),
        out_specs=P(("dp", "expert"), None, None),
        check_vma=False,
    )
```

time: 60.9 us -> 47.2 us (0.78)
  Pallas kernels: 58.9 us -> 47.2 us
  local copies, waits for them, and re-layouts: 1.87 us -> 0 us
    pallas_call x1, Pallas kernels: 57.8 us -> 46.1 us  [shards(): pl.pallas_call(kernel, out_shape=[pltpu.VMEM((m, n_ex), bf16), pltpu.VMEM...]
    unnamed x1 -> x0, local copies, waits for them, and re-layouts: 1.87 us -> none
where the time goes in v1:
time: 47.2 us
  Pallas kernels  47.2 us (100%)
    pallas_call x1, Pallas kernels, shards(): pl.pallas_call(kernel, out_shape=[pltpu.VMEM((m, n_ex), bf16), pltpu.VMEM...  46.1 us
    pallas_call x1, Pallas kernels, shards(): pl.pallas_call(mix_kernel, out_shape=jax.ShapeDtypeStruct(tokens.shape, b...  1.08 us

profile of v1, /device:TPU:1, one launch (start us, length us, event | category | flops | bytes accessed | tf_op | source)
XLA Modules:
  0.0 47.2 jit_solution(15919147507899184450)
XLA Ops:
  0.0 46.1 %shard_map.64 = (bf16[256,128]{1,0:T(8,128)(2,1)S(1)}, bf16[128,1280]{1,0:T(8,128)(2,1)S(1)}) custom-call(bf16[1,256,1280]{2,1,0:T(8,128)(2,1)} %tokens_hbm.1, bf16[1280,128]{1,0:T(8,128)(2,1)} %router_hbm.1, bf16[1,1280,2560]{2,1,0:T(8,128)(2,1)} %w_in_hbm.1, bf16[1,5120]{1,0:T(2,128)(2,1)} %b_in_hbm.1, bf16[1,2560,1280]{2,1,0:T(8,128)(2,1)} %w_out_hbm.1, ...), custom_call_target="tpu_custom_call" | custom-call | tf_op jit(solution)/shard_map/pallas_call | solution.py:294
  46.1 1.1 %shard_map.65 = bf16[1,256,1280]{2,1,0:T(8,128)(2,1)} custom-call(bf16[256,128]{1,0:T(8,128)(2,1)S(1)} %get-tuple-element.7.combine, bf16[128,1280]{1,0:T(8,128)(2,1)S(1)} %get-tuple-element.8.expert_out), custom_call_target="tpu_custom_call" | custom-call | tf_op jit(solution)/shard_map/pallas_call | solution.py:337

commit v2 on v1

--- a/solution.py
+++ b/solution.py
@@ -13,9 +13,12 @@
 NY, NZ, QUAD = 4, 8, 4
 NQ = NY * QUAD
 NP = 2 * NQ
-SENDS_ORDER = (4, 3, 5, 2, 6, 1, 7)
+COLUMN = (4, 3, 5, 2, 6, 1, 7)
 FORWARD_ORDER = (0, 4, 3, 5, 2, 6, 1, 7)
-REDUCE_ORDER = (4, 3, 5, 2, 6, 1, 7, 0)
+BATCHES = ((0, 4, 3, 5), (2, 6, 1, 7))
+SCATTERS = ((4, 3, 5), (2, 6, 1, 7, 0))
+REDUCE_ORDER = (4, 3, 5, 2, 6, 0)
+DIRECT = (1, 7)
 
 
 def gelu(v):
@@ -62,7 +65,7 @@
     z_sems,
     plane1_sems,
     plane2_sems,
-    eo_sem,
+    eo_sems,
 ):
     me_dp = lax.axis_index("dp")
     me_ex = lax.axis_index("expert")
@@ -83,13 +86,14 @@
     quads = [lax.rem(me_xh + dx, 2) * 2 + lax.rem(me_core + dc, 2) for dc in range(2) for dx in range(2)]
     dps = [me_dp, 1 - me_dp]
     plane = []
-    for t in range(NP - 1, 0, -1):
+    for t in range(NP - 1, -1, -1):
         y, a, quad = ys[t % NY], dps[t // NY % 2], quads[t // (2 * NY)]
-        plane.append((a, y * QUAD + quad, (a, y * (NZ * QUAD) + me_z * QUAD + quad)))
-
-    def each_in_plane(action):
-        for target in plane:
-            action(*target)
+        plane.append((a, y * QUAD + quad, y * (NZ * QUAD) + quad))
+
+    def each_in_plane(d, action):
+        z = lax.rem(me_z + d, NZ) * QUAD
+        for a, q, ex in plane if d else plane[:-1]:
+            action(a, q, (a, ex + z))
 
     def remote(src, dst, send_sem, recv_sem, device):
         pltpu.make_async_remote_copy(
@@ -115,9 +119,9 @@
         pl.semaphore_signal(barrier, inc=1, device_id=device, device_id_type=MESH)
 
     with jax.named_scope("greet"):
-        for d in SENDS_ORDER:
+        for d in COLUMN:
             greet(along_z(d)[1])
-        each_in_plane(lambda a, q, device: greet(device))
+        each_in_plane(0, lambda a, q, device: greet(device))
 
     def pieces(hbm, vmem, sems):
         count = sems.shape[0]
@@ -152,7 +156,7 @@
         pl.semaphore_wait(barrier, NZ - 1 + NP - 1)
 
     with jax.named_scope("sendz"):
-        for d in SENDS_ORDER:
+        for d in COLUMN:
             z, device = along_z(d)
             back = NZ - d
             remote(
@@ -182,7 +186,7 @@
                 device,
             )
 
-        each_in_plane(send)
+        each_in_plane(0, send)
         recv1[r, me_p] = fwd[r, me_q]
 
     with jax.named_scope("combine"):
@@ -194,37 +198,18 @@
         with jax.named_scope("forward%d" % r):
             forward(r)
 
-    for r in FORWARD_ORDER:
-        with jax.named_scope("recv1_%d" % r):
+    half = w_in.shape[1]
+    tile = 2 * LANES
+    keep = (me_dp == 0).astype(jnp.float32)
+
+    def gather(r, at):
+        with jax.named_scope("gather%d" % r):
             wait_copy(recv1.at[r, pl.ds(0, NP - 1), pl.ds(0, chunks)], plane1_sems.at[r])
             wide32[...] = recv1[r].astype(jnp.float32).reshape(wide32.shape)
             for j in range(chunks):
-                x_ref[r * NP : (r + 1) * NP, j * LANES : (j + 1) * LANES] = wide32[
+                x_ref[at : at + NP, j * LANES : (j + 1) * LANES] = wide32[
                     pl.ds(j, NP, stride=PITCH), :
                 ].astype(jnp.bfloat16)
-
-    for load in loads[2:] + w_in_loads:
-        load.wait()
-    half = w_in.shape[1]
-    tile = 2 * LANES
-
-    with jax.named_scope("mlp1"):
-        for at in range(0, half, tile):
-            bias = b_in[:, pl.ds(pl.multiple_of(me_dp * half + at, LANES), tile)].astype(jnp.float32)
-            v = jnp.dot(x_ref[...], w_in[:, at : at + tile], preferred_element_type=jnp.float32) + bias
-            hid[:, at : at + tile] = gelu(v).astype(jnp.bfloat16)
-
-    for load in w_out_loads:
-        load.wait()
-    keep = (me_dp == 0).astype(jnp.float32)
-    n = NZ * NP
-    with jax.named_scope("mlp2"):
-        for at in range(0, width, tile):
-            y = jnp.dot(hid[...], w_out[:, at : at + tile], preferred_element_type=jnp.float32)
-            y = y + keep * b_out[:, at : at + tile].astype(jnp.float32)
-            for c in range(tile // LANES):
-                wide_rows[pl.ds(at // LANES + c, n, stride=PITCH), :] = y[:, c * LANES : (c + 1) * LANES]
-        send2[...] = wide_rows[...].reshape(send2.shape).astype(jnp.bfloat16)
 
     def scatter(r):
         def send(a, q, device):
@@ -236,35 +221,80 @@
                 device,
             )
 
-        each_in_plane(send)
-        recv2[r, me_p] = send2[r, me_p]
-
-    with jax.named_scope("scatter"):
-        for r in REDUCE_ORDER:
-            scatter(r)
+        each_in_plane(r if r in DIRECT else 0, send)
+
+    start = 0
+    for batch, leaving in zip(BATCHES, SCATTERS, strict=True):
+        n = len(batch) * NP
+        rows = slice(start, start + n)
+        for i, r in enumerate(batch):
+            gather(r, start + i * NP)
+        if start == 0:
+            for load in loads[2:] + w_in_loads:
+                load.wait()
+        with jax.named_scope("mlp1_%d" % start):
+            for at in range(0, half, tile):
+                bias = b_in[:, pl.ds(pl.multiple_of(me_dp * half + at, LANES), tile)].astype(jnp.float32)
+                v = jnp.dot(x_ref[rows, :], w_in[:, at : at + tile], preferred_element_type=jnp.float32) + bias
+                hid[rows, at : at + tile] = gelu(v).astype(jnp.bfloat16)
+        if start == 0:
+            for load in w_out_loads:
+                load.wait()
+        with jax.named_scope("mlp2_%d" % start):
+            for at in range(0, width, tile):
+                y = jnp.dot(hid[rows, :], w_out[:, at : at + tile], preferred_element_type=jnp.float32)
+                y = y + keep * b_out[:, at : at + tile].astype(jnp.float32)
+                for c in range(tile // LANES):
+                    wide_rows[pl.ds(start * PITCH + at // LANES + c, n, stride=PITCH), :] = y[
+                        :, c * LANES : (c + 1) * LANES
+                    ]
+        with jax.named_scope("scatter_%d" % start):
+            for r in sorted(batch, key=(leaving + (0,)).index):
+                first = (start + batch.index(r) * NP) * PITCH
+                send2[r] = wide_rows[first : first + NP * PITCH, :].reshape(NP, PITCH, LANES).astype(jnp.bfloat16)
+                if r not in DIRECT:
+                    recv2[r, me_p] = send2[r, me_p]
+            for r in leaving:
+                scatter(r)
+        start += n
+
+    def reduce(r):
+        rows = NP if r in DIRECT else NP - 1
+        wait_copy(recv2.at[r, pl.ds(0, rows), pl.ds(0, chunks)], plane2_sems.at[r])
+        pair = recv2[r, :NQ].astype(jnp.float32) + recv2[r, NQ:].astype(jnp.float32)
+        wide16[r] = pair.reshape(NQ * PITCH, LANES)
+        for j in range(chunks):
+            total[r, :, j * LANES : (j + 1) * LANES] = wide16[r, pl.ds(j, NQ, stride=PITCH), :].astype(jnp.bfloat16)
+
+    def expert_rows(z):
+        return pl.ds(pl.multiple_of(z * NQ, NQ), NQ)
 
     for r in REDUCE_ORDER:
         with jax.named_scope("reduce%d" % r):
-            wait_copy(recv2.at[r, pl.ds(0, NP - 1), pl.ds(0, chunks)], plane2_sems.at[r])
-            pair = recv2[r, :NQ].astype(jnp.float32) + recv2[r, NQ:].astype(jnp.float32)
-            wide16[r] = pair.reshape(NQ * PITCH, LANES)
-            for j in range(chunks):
-                total[r, :, j * LANES : (j + 1) * LANES] = wide16[r, pl.ds(j, NQ, stride=PITCH), :].astype(jnp.bfloat16)
-            mine = pl.ds(pl.multiple_of(me_z * NQ, NQ), NQ)
+            reduce(r)
             if r == 0:
-                eland[mine, :] = total[r]
+                eland[0] = total[0]
             else:
-                remote(total.at[r], eland.at[mine], send_sems.at[3], eo_sem, along_z(r)[1])
-
-    with jax.named_scope("recv2"):
-        wait_copy(eland.at[pl.ds(0, (NZ - 1) * NQ)], eo_sem)
+                remote(total.at[r], eland.at[NZ - r], send_sems.at[3], eo_sems.at[NZ - r], along_z(r)[1])
+    for r in DIRECT:
+        with jax.named_scope("direct%d" % r):
+            reduce(r)
+            eland[NZ - r] = total[r]
+
+    for r in (4, 3, 5, 2, 6, 1, 7, 0):
+        with jax.named_scope("eo%d" % r):
+            back = (NZ - r) % NZ
+            if r and r not in DIRECT:
+                wait_copy(eland.at[back], eo_sems.at[back])
+            eo[expert_rows(lax.rem(me_z + back, NZ)), :] = eland[back]
     with jax.named_scope("tail"):
-        eo[...] = eland[...]
-        rows = recv1.at[:, pl.ds(0, NP - 1), pl.ds(0, chunks)]
+        sent = recv1.at[:, pl.ds(0, NP - 1), pl.ds(0, chunks)]
+        wait_copy(sent, send_sems.at[1])
+        wait_copy(sent, send_sems.at[2])
+        for r in DIRECT:
+            wait_copy(recv1.at[r, 0, pl.ds(0, chunks)], send_sems.at[2])
         wait_copy(zland.at[pl.ds(0, NZ - 1)], send_sems.at[0])
-        wait_copy(rows, send_sems.at[1])
-        wait_copy(rows, send_sems.at[2])
-        wait_copy(zland.at[pl.ds(0, NZ - 1)], send_sems.at[3])
+        wait_copy(zland.at[pl.ds(0, len(REDUCE_ORDER) - 1)], send_sems.at[3])
 
 
 def mix_kernel(combine, expert_out, out_hbm, mixed, sems):
@@ -319,7 +349,7 @@
             pltpu.VMEM((NZ, NP, PITCH, LANES), bf16),
             pltpu.VMEM((NZ, NP, PITCH, LANES), bf16),
             pltpu.VMEM((NZ, NQ, width), bf16),
-            pltpu.VMEM((n_ex, width), bf16),
+            pltpu.VMEM((NZ, NQ, width), bf16),
             dma((4,)),
             dma((4,)),
             dma((4,)),
@@ -327,7 +357,7 @@
             dma((NZ,)),
             dma((NZ,)),
             dma((NZ,)),
-            dma,
+            dma((NZ,)),
         ],
         compiler_params=pltpu.CompilerParams(
             collective_id=0, has_side_effects=True, vmem_limit_bytes=60 * 1024 * 1024

time: 47.2 us -> 42.3 us (0.90)
  Pallas kernels: 47.2 us -> 42.2 us
    pallas_call x1, Pallas kernels: 46.1 us -> 41.2 us  [shards(): pl.pallas_call(kernel, out_shape=[pltpu.VMEM((m, n_ex), bf16), pltpu.VMEM...]
where the time goes in v2:
time: 42.3 us
  Pallas kernels  42.2 us (100%)
    pallas_call x1, Pallas kernels, shards(): pl.pallas_call(kernel, out_shape=[pltpu.VMEM((m, n_ex), bf16), pltpu.VMEM...  41.2 us
    pallas_call x1, Pallas kernels, shards(): pl.pallas_call(mix_kernel, out_shape=jax.ShapeDtypeStruct(tokens.shape, b...  1.08 us

profile of v2, /device:TPU:1, one launch (start us, length us, event | category | flops | bytes accessed | tf_op | source)
XLA Modules:
  0.0 42.3 jit_solution(6777176949329490647)
XLA Ops:
  0.0 41.2 %shard_map.64 = (bf16[256,128]{1,0:T(8,128)(2,1)S(1)}, bf16[128,1280]{1,0:T(8,128)(2,1)S(1)}) custom-call(bf16[1,256,1280]{2,1,0:T(8,128)(2,1)} %tokens_hbm.1, bf16[1280,128]{1,0:T(8,128)(2,1)} %router_hbm.1, bf16[1,1280,2560]{2,1,0:T(8,128)(2,1)} %w_in_hbm.1, bf16[1,5120]{1,0:T(2,128)(2,1)} %b_in_hbm.1, bf16[1,2560,1280]{2,1,0:T(8,128)(2,1)} %w_out_hbm.1, ...), custom_call_target="tpu_custom_call" | custom-call | tf_op jit(solution)/shard_map/pallas_call | solution.py:324
  41.2 1.1 %shard_map.65 = bf16[1,256,1280]{2,1,0:T(8,128)(2,1)} custom-call(bf16[256,128]{1,0:T(8,128)(2,1)S(1)} %get-tuple-element.7.combine, bf16[128,1280]{1,0:T(8,128)(2,1)S(1)} %get-tuple-element.8.expert_out), custom_call_target="tpu_custom_call" | custom-call | tf_op jit(solution)/shard_map/pallas_call | solution.py:367

commit v3 on v1

--- a/solution.py
+++ b/solution.py
@@ -13,9 +13,10 @@
 NY, NZ, QUAD = 4, 8, 4
 NQ = NY * QUAD
 NP = 2 * NQ
-SENDS_ORDER = (4, 3, 5, 2, 6, 1, 7)
-FORWARD_ORDER = (0, 4, 3, 5, 2, 6, 1, 7)
-REDUCE_ORDER = (4, 3, 5, 2, 6, 1, 7, 0)
+COLUMN = (4, 1, 7, 2, 6, 3, 5)
+BATCHES = ((0, 4, 1, 7), (3, 5, 2, 6))
+DIRECT = ()
+STEPS = "f0 f4 f1 f7 f2 f6 f3 f5 g0 g4 g1 g7 m0 s4 s1 s7 g3 g5 g2 g6 m1 s3 s5 r4 r1 r7 s2 s6 s0 r3 r5 r2 r6 r0".split()
 
 
 def gelu(v):
@@ -56,9 +57,7 @@
     total,
     eland,
     load_sems,
-    w_in_sems,
-    w_out_sems,
-    send_sems,
+    send_sem,
     z_sems,
     plane1_sems,
     plane2_sems,
@@ -83,13 +82,14 @@
     quads = [lax.rem(me_xh + dx, 2) * 2 + lax.rem(me_core + dc, 2) for dc in range(2) for dx in range(2)]
     dps = [me_dp, 1 - me_dp]
     plane = []
-    for t in range(NP - 1, 0, -1):
+    for t in range(NP - 1, -1, -1):
         y, a, quad = ys[t % NY], dps[t // NY % 2], quads[t // (2 * NY)]
-        plane.append((a, y * QUAD + quad, (a, y * (NZ * QUAD) + me_z * QUAD + quad)))
-
-    def each_in_plane(action):
-        for target in plane:
-            action(*target)
+        plane.append((a, y * QUAD + quad, y * (NZ * QUAD) + quad))
+
+    def each_in_plane(d, action):
+        z = lax.rem(me_z + d, NZ) * QUAD
+        for a, q, ex in plane if d else plane[:-1]:
+            action(a, q, (a, ex + z))
 
     def remote(src, dst, send_sem, recv_sem, device):
         pltpu.make_async_remote_copy(
@@ -103,9 +103,11 @@
 
     loads = [
         pltpu.make_async_copy(tokens_hbm.at[0], tok, load_sems.at[0]),
-        pltpu.make_async_copy(router_hbm, router, load_sems.at[1]),
-        pltpu.make_async_copy(b_in_hbm, b_in, load_sems.at[2]),
-        pltpu.make_async_copy(b_out_hbm, b_out, load_sems.at[3]),
+        pltpu.make_async_copy(router_hbm, router, load_sems.at[0]),
+        pltpu.make_async_copy(w_in_hbm.at[0], w_in, load_sems.at[1]),
+        pltpu.make_async_copy(b_in_hbm, b_in, load_sems.at[1]),
+        pltpu.make_async_copy(w_out_hbm.at[0], w_out, load_sems.at[1]),
+        pltpu.make_async_copy(b_out_hbm, b_out, load_sems.at[1]),
     ]
     loads[0].start()
     loads[1].start()
@@ -115,23 +117,11 @@
         pl.semaphore_signal(barrier, inc=1, device_id=device, device_id_type=MESH)
 
     with jax.named_scope("greet"):
-        for d in SENDS_ORDER:
+        for d in COLUMN:
             greet(along_z(d)[1])
-        each_in_plane(lambda a, q, device: greet(device))
-
-    def pieces(hbm, vmem, sems):
-        count = sems.shape[0]
-        rows = vmem.shape[0] // count
-        return [
-            pltpu.make_async_copy(
-                hbm.at[0, pl.ds(i * rows, rows)], vmem.at[pl.ds(i * rows, rows)], sems.at[i]
-            )
-            for i in range(count)
-        ]
-
-    w_in_loads = pieces(w_in_hbm, w_in, w_in_sems)
-    w_out_loads = pieces(w_out_hbm, w_out, w_out_sems)
-    for load in w_in_loads + loads[2:] + w_out_loads:
+        each_in_plane(0, lambda a, q, device: greet(device))
+
+    for load in loads[2:]:
         load.start()
 
     with jax.named_scope("waittok"):
@@ -152,13 +142,13 @@
         pl.semaphore_wait(barrier, NZ - 1 + NP - 1)
 
     with jax.named_scope("sendz"):
-        for d in SENDS_ORDER:
+        for d in COLUMN:
             z, device = along_z(d)
             back = NZ - d
             remote(
                 send1.at[pl.ds(pl.multiple_of(z * NQ, NQ), NQ)],
                 zland.at[back],
-                send_sems.at[0],
+                send_sem,
                 z_sems.at[back],
                 device,
             )
@@ -177,12 +167,12 @@
             remote(
                 fwd.at[r, q, pl.ds(0, chunks)],
                 recv1.at[r, me_p, pl.ds(0, chunks)],
-                send_sems.at[1],
+                send_sem,
                 plane1_sems.at[r],
                 device,
             )
 
-        each_in_plane(send)
+        each_in_plane(0, send)
         recv1[r, me_p] = fwd[r, me_q]
 
     with jax.named_scope("combine"):
@@ -190,81 +180,89 @@
         combine = over_experts / jnp.sum(over_experts, axis=0, keepdims=True)
         comb_ref[...] = combine.T.astype(jnp.bfloat16)
 
-    for r in FORWARD_ORDER:
-        with jax.named_scope("forward%d" % r):
-            forward(r)
-
-    for r in FORWARD_ORDER:
-        with jax.named_scope("recv1_%d" % r):
-            wait_copy(recv1.at[r, pl.ds(0, NP - 1), pl.ds(0, chunks)], plane1_sems.at[r])
-            wide32[...] = recv1[r].astype(jnp.float32).reshape(wide32.shape)
-            for j in range(chunks):
-                x_ref[r * NP : (r + 1) * NP, j * LANES : (j + 1) * LANES] = wide32[
-                    pl.ds(j, NP, stride=PITCH), :
-                ].astype(jnp.bfloat16)
-
-    for load in loads[2:] + w_in_loads:
-        load.wait()
     half = w_in.shape[1]
     tile = 2 * LANES
-
-    with jax.named_scope("mlp1"):
+    keep = (me_dp == 0).astype(jnp.float32)
+
+    def gather(r):
+        at = order.index(r) * NP
+        wait_copy(recv1.at[r, pl.ds(0, NP - 1), pl.ds(0, chunks)], plane1_sems.at[r])
+        wide32[...] = recv1[r].astype(jnp.float32).reshape(wide32.shape)
+        for j in range(chunks):
+            x_ref[at : at + NP, j * LANES : (j + 1) * LANES] = wide32[
+                pl.ds(j, NP, stride=PITCH), :
+            ].astype(jnp.bfloat16)
+
+    def multiply(batch):
+        start = order.index(BATCHES[batch][0]) * NP
+        n = len(BATCHES[batch]) * NP
+        rows = slice(start, start + n)
+        if batch == 0:
+            for load in loads[2:]:
+                load.wait()
         for at in range(0, half, tile):
             bias = b_in[:, pl.ds(pl.multiple_of(me_dp * half + at, LANES), tile)].astype(jnp.float32)
-            v = jnp.dot(x_ref[...], w_in[:, at : at + tile], preferred_element_type=jnp.float32) + bias
-            hid[:, at : at + tile] = gelu(v).astype(jnp.bfloat16)
-
-    for load in w_out_loads:
-        load.wait()
-    keep = (me_dp == 0).astype(jnp.float32)
-    n = NZ * NP
-    with jax.named_scope("mlp2"):
+            v = jnp.dot(x_ref[rows, :], w_in[:, at : at + tile], preferred_element_type=jnp.float32) + bias
+            hid[rows, at : at + tile] = gelu(v).astype(jnp.bfloat16)
         for at in range(0, width, tile):
-            y = jnp.dot(hid[...], w_out[:, at : at + tile], preferred_element_type=jnp.float32)
+            y = jnp.dot(hid[rows, :], w_out[:, at : at + tile], preferred_element_type=jnp.float32)
             y = y + keep * b_out[:, at : at + tile].astype(jnp.float32)
             for c in range(tile // LANES):
-                wide_rows[pl.ds(at // LANES + c, n, stride=PITCH), :] = y[:, c * LANES : (c + 1) * LANES]
-        send2[...] = wide_rows[...].reshape(send2.shape).astype(jnp.bfloat16)
+                wide_rows[pl.ds(start * PITCH + at // LANES + c, n, stride=PITCH), :] = y[
+                    :, c * LANES : (c + 1) * LANES
+                ]
+        for r in BATCHES[batch]:
+            first = order.index(r) * NP * PITCH
+            send2[r] = wide_rows[first : first + NP * PITCH, :].reshape(NP, PITCH, LANES).astype(jnp.bfloat16)
 
     def scatter(r):
         def send(a, q, device):
             remote(
                 send2.at[r, a * NQ + q, pl.ds(0, chunks)],
                 recv2.at[r, me_p, pl.ds(0, chunks)],
-                send_sems.at[2],
+                send_sem,
                 plane2_sems.at[r],
                 device,
             )
 
-        each_in_plane(send)
-        recv2[r, me_p] = send2[r, me_p]
-
-    with jax.named_scope("scatter"):
-        for r in REDUCE_ORDER:
-            scatter(r)
-
-    for r in REDUCE_ORDER:
-        with jax.named_scope("reduce%d" % r):
-            wait_copy(recv2.at[r, pl.ds(0, NP - 1), pl.ds(0, chunks)], plane2_sems.at[r])
-            pair = recv2[r, :NQ].astype(jnp.float32) + recv2[r, NQ:].astype(jnp.float32)
-            wide16[r] = pair.reshape(NQ * PITCH, LANES)
-            for j in range(chunks):
-                total[r, :, j * LANES : (j + 1) * LANES] = wide16[r, pl.ds(j, NQ, stride=PITCH), :].astype(jnp.bfloat16)
-            mine = pl.ds(pl.multiple_of(me_z * NQ, NQ), NQ)
-            if r == 0:
-                eland[mine, :] = total[r]
-            else:
-                remote(total.at[r], eland.at[mine], send_sems.at[3], eo_sem, along_z(r)[1])
-
-    with jax.named_scope("recv2"):
-        wait_copy(eland.at[pl.ds(0, (NZ - 1) * NQ)], eo_sem)
+        each_in_plane(r if r in DIRECT else 0, send)
+        if r not in DIRECT:
+            recv2[r, me_p] = send2[r, me_p]
+
+    def reduce(r):
+        rows = NP if r in DIRECT else NP - 1
+        wait_copy(recv2.at[r, pl.ds(0, rows), pl.ds(0, chunks)], plane2_sems.at[r])
+        pair = recv2[r, :NQ].astype(jnp.float32) + recv2[r, NQ:].astype(jnp.float32)
+        wide16[r] = pair.reshape(NQ * PITCH, LANES)
+        for j in range(chunks):
+            total[r, :, j * LANES : (j + 1) * LANES] = wide16[r, pl.ds(j, NQ, stride=PITCH), :].astype(jnp.bfloat16)
+        back = (NZ - r) % NZ
+        if r == 0 or r in DIRECT:
+            eo[expert_rows(back), :] = total[r]
+        else:
+            remote(total.at[r], eland.at[back], send_sem, eo_sem, along_z(r)[1])
+
+    def expert_rows(d):
+        return pl.ds(pl.multiple_of(lax.rem(me_z + d, NZ) * NQ, NQ), NQ)
+
+    order = sum(BATCHES, ())
+    actions = {"f": forward, "g": gather, "m": multiply, "s": scatter, "r": reduce}
+    for step in STEPS:
+        with jax.named_scope(step):
+            actions[step[0]](int(step[1]))
+
+    relayed = [r for r in COLUMN if r not in DIRECT]
+    with jax.named_scope("eo"):
+        wait_copy(zland.at[pl.ds(0, len(relayed))], eo_sem)
+        for r in relayed:
+            eo[expert_rows(NZ - r), :] = eland[NZ - r]
     with jax.named_scope("tail"):
-        eo[...] = eland[...]
-        rows = recv1.at[:, pl.ds(0, NP - 1), pl.ds(0, chunks)]
-        wait_copy(zland.at[pl.ds(0, NZ - 1)], send_sems.at[0])
-        wait_copy(rows, send_sems.at[1])
-        wait_copy(rows, send_sems.at[2])
-        wait_copy(zland.at[pl.ds(0, NZ - 1)], send_sems.at[3])
+        for sent in (recv1, recv2):
+            wait_copy(sent.at[:, pl.ds(0, NP - 1), pl.ds(0, chunks)], send_sem)
+        for r in DIRECT:
+            wait_copy(recv1.at[r, 0, pl.ds(0, chunks)], send_sem)
+        wait_copy(zland.at[pl.ds(0, NZ - 1)], send_sem)
+        wait_copy(zland.at[pl.ds(0, len(relayed))], send_sem)
 
 
 def mix_kernel(combine, expert_out, out_hbm, mixed, sems):
@@ -319,11 +317,9 @@
             pltpu.VMEM((NZ, NP, PITCH, LANES), bf16),
             pltpu.VMEM((NZ, NP, PITCH, LANES), bf16),
             pltpu.VMEM((NZ, NQ, width), bf16),
-            pltpu.VMEM((n_ex, width), bf16),
-            dma((4,)),
-            dma((4,)),
-            dma((4,)),
-            dma((4,)),
+            pltpu.VMEM((NZ, NQ, width), bf16),
+            dma((2,)),
+            dma,
             dma((NZ,)),
             dma((NZ,)),
             dma((NZ,)),

time: 47.2 us -> 41.1 us (0.87)
  Pallas kernels: 47.2 us -> 41 us
    pallas_call x1, Pallas kernels: 46.1 us -> 39.9 us  [shards(): pl.pallas_call(kernel, out_shape=[pltpu.VMEM((m, n_ex), bf16), pltpu.VMEM...]
where the time goes in v3:
time: 41.1 us; the launch traced here: 41 us
  Pallas kernels  41 us (100%)
    pallas_call x1, Pallas kernels, shards(): pl.pallas_call(kernel, out_shape=[pltpu.VMEM((m, n_ex), bf16), pltpu.VMEM...  39.9 us
    pallas_call x1, Pallas kernels, shards(): pl.pallas_call(mix_kernel, out_shape=jax.ShapeDtypeStruct(tokens.shape, b...  1.08 us

profile of v3, /device:TPU:1, one launch (start us, length us, event | category | flops | bytes accessed | tf_op | source)
XLA Modules:
  0.0 41.0 jit_solution(1018501395557362703)
XLA Ops:
  0.0 39.9 %shard_map.64 = (bf16[256,128]{1,0:T(8,128)(2,1)S(1)}, bf16[128,1280]{1,0:T(8,128)(2,1)S(1)}) custom-call(bf16[1,256,1280]{2,1,0:T(8,128)(2,1)} %tokens_hbm.1, bf16[1280,128]{1,0:T(8,128)(2,1)} %router_hbm.1, bf16[1,1280,2560]{2,1,0:T(8,128)(2,1)} %w_in_hbm.1, bf16[1,5120]{1,0:T(2,128)(2,1)} %b_in_hbm.1, bf16[1,2560,1280]{2,1,0:T(8,128)(2,1)} %w_out_hbm.1, ...), custom_call_target="tpu_custom_call" | custom-call | tf_op jit(solution)/shard_map/pallas_call | solution.py:292
  39.9 1.1 %shard_map.65 = bf16[1,256,1280]{2,1,0:T(8,128)(2,1)} custom-call(bf16[256,128]{1,0:T(8,128)(2,1)S(1)} %get-tuple-element.7.combine, bf16[128,1280]{1,0:T(8,128)(2,1)S(1)} %get-tuple-element.8.expert_out), custom_call_target="tpu_custom_call" | custom-call | tf_op jit(solution)/shard_map/pallas_call | solution.py:333

commit v4 on v3

--- a/solution.py
+++ b/solution.py
@@ -16,7 +16,9 @@
 COLUMN = (4, 1, 7, 2, 6, 3, 5)
 BATCHES = ((0, 4, 1, 7), (3, 5, 2, 6))
 DIRECT = ()
-STEPS = "f0 f4 f1 f7 f2 f6 f3 f5 g0 g4 g1 g7 m0 s4 s1 s7 g3 g5 g2 g6 m1 s3 s5 r4 r1 r7 s2 s6 s0 r3 r5 r2 r6 r0".split()
+STEPS = ("f0", "f4", "f1", "f7", "f2", "f6", "f3", "f5", "g0", "g4", "g1", "g7", "m0", "s4", "s1", "s7", "g3", "g5", "g2", "g6", "m1", "s3", "s5", "r4", "r1", "r7", "s2", "s6", "s0", "r3", "r5", "r2", "r6", "r0")
+TILE1 = 256
+TILE2 = 256
 
 
 def gelu(v):
@@ -181,7 +183,6 @@
         comb_ref[...] = combine.T.astype(jnp.bfloat16)
 
     half = w_in.shape[1]
-    tile = 2 * LANES
     keep = (me_dp == 0).astype(jnp.float32)
 
     def gather(r):
@@ -200,22 +201,22 @@
         if batch == 0:
             for load in loads[2:]:
                 load.wait()
-        for at in range(0, half, tile):
-            bias = b_in[:, pl.ds(pl.multiple_of(me_dp * half + at, LANES), tile)].astype(jnp.float32)
-            v = jnp.dot(x_ref[rows, :], w_in[:, at : at + tile], preferred_element_type=jnp.float32) + bias
-            hid[rows, at : at + tile] = gelu(v).astype(jnp.bfloat16)
-        for at in range(0, width, tile):
-            y = jnp.dot(hid[rows, :], w_out[:, at : at + tile], preferred_element_type=jnp.float32)
-            y = y + keep * b_out[:, at : at + tile].astype(jnp.float32)
-            for c in range(tile // LANES):
+        for at in range(0, half, TILE1):
+            bias = b_in[:, pl.ds(pl.multiple_of(me_dp * half + at, LANES), TILE1)].astype(jnp.float32)
+            v = jnp.dot(x_ref[rows, :], w_in[:, at : at + TILE1], preferred_element_type=jnp.float32) + bias
+            hid[rows, at : at + TILE1] = gelu(v).astype(jnp.bfloat16)
+        for at in range(0, width, TILE2):
+            y = jnp.dot(hid[rows, :], w_out[:, at : at + TILE2], preferred_element_type=jnp.float32)
+            y = y + keep * b_out[:, at : at + TILE2].astype(jnp.float32)
+            for c in range(TILE2 // LANES):
                 wide_rows[pl.ds(start * PITCH + at // LANES + c, n, stride=PITCH), :] = y[
                     :, c * LANES : (c + 1) * LANES
                 ]
-        for r in BATCHES[batch]:
-            first = order.index(r) * NP * PITCH
-            send2[r] = wide_rows[first : first + NP * PITCH, :].reshape(NP, PITCH, LANES).astype(jnp.bfloat16)
 
     def scatter(r):
+        first = order.index(r) * NP * PITCH
+        send2[r] = wide_rows[first : first + NP * PITCH, :].reshape(NP, PITCH, LANES).astype(jnp.bfloat16)
+
         def send(a, q, device):
             remote(
                 send2.at[r, a * NQ + q, pl.ds(0, chunks)],

time: 41.1 us -> 41.1 us (level)
  no operation moved by 1% of the time
where the time goes in v4:
time: 41.1 us; the launch traced here: 41 us
  Pallas kernels  41 us (100%)
    pallas_call x1, Pallas kernels, shards(): pl.pallas_call(kernel, out_shape=[pltpu.VMEM((m, n_ex), bf16), pltpu.VMEM...  39.9 us
    pallas_call x1, Pallas kernels, shards(): pl.pallas_call(mix_kernel, out_shape=jax.ShapeDtypeStruct(tokens.shape, b...  1.08 us

profile of v4, /device:TPU:1, one launch (start us, length us, event | category | flops | bytes accessed | tf_op | source)
XLA Modules:
  0.0 41.0 jit_solution(1533609503885494418)
XLA Ops:
  0.0 39.9 %shard_map.64 = (bf16[256,128]{1,0:T(8,128)(2,1)S(1)}, bf16[128,1280]{1,0:T(8,128)(2,1)S(1)}) custom-call(bf16[1,256,1280]{2,1,0:T(8,128)(2,1)} %tokens_hbm.1, bf16[1280,128]{1,0:T(8,128)(2,1)} %router_hbm.1, bf16[1,1280,2560]{2,1,0:T(8,128)(2,1)} %w_in_hbm.1, bf16[1,5120]{1,0:T(2,128)(2,1)} %b_in_hbm.1, bf16[1,2560,1280]{2,1,0:T(8,128)(2,1)} %w_out_hbm.1, ...), custom_call_target="tpu_custom_call" | custom-call | tf_op jit(solution)/shard_map/pallas_call | solution.py:293
  39.9 1.1 %shard_map.65 = bf16[1,256,1280]{2,1,0:T(8,128)(2,1)} custom-call(bf16[256,128]{1,0:T(8,128)(2,1)S(1)} %get-tuple-element.7.combine, bf16[128,1280]{1,0:T(8,128)(2,1)S(1)} %get-tuple-element.8.expert_out), custom_call_target="tpu_custom_call" | custom-call | tf_op jit(solution)/shard_map/pallas_call | solution.py:334

commit v5 on v4

--- a/solution.py
+++ b/solution.py
@@ -17,6 +17,8 @@
 BATCHES = ((0, 4, 1, 7), (3, 5, 2, 6))
 DIRECT = ()
 STEPS = ("f0", "f4", "f1", "f7", "f2", "f6", "f3", "f5", "g0", "g4", "g1", "g7", "m0", "s4", "s1", "s7", "g3", "g5", "g2", "g6", "m1", "s3", "s5", "r4", "r1", "r7", "s2", "s6", "s0", "r3", "r5", "r2", "r6", "r0")
+FAR = True
+MIX_TILES = 4
 TILE1 = 256
 TILE2 = 256
 
@@ -84,13 +86,17 @@
     quads = [lax.rem(me_xh + dx, 2) * 2 + lax.rem(me_core + dc, 2) for dc in range(2) for dx in range(2)]
     dps = [me_dp, 1 - me_dp]
     plane = []
-    for t in range(NP - 1, -1, -1):
+    def hops(t):
+        dy, da, dx = t % NY, t // NY % 2, t // (2 * NY) % 2
+        return min(dy, NY - dy) + (1 if da else 2 * dx)
+
+    for t in sorted(range(NP - 1, -1, -1), key=hops, reverse=FAR):
         y, a, quad = ys[t % NY], dps[t // NY % 2], quads[t // (2 * NY)]
         plane.append((a, y * QUAD + quad, y * (NZ * QUAD) + quad))
 
     def each_in_plane(d, action):
         z = lax.rem(me_z + d, NZ) * QUAD
-        for a, q, ex in plane if d else plane[:-1]:
+        for a, q, ex in plane[:-1]:
             action(a, q, (a, ex + z))
 
     def remote(src, dst, send_sem, recv_sem, device):
@@ -268,14 +274,14 @@
 
 def mix_kernel(combine, expert_out, out_hbm, mixed, sems):
     count = sems.shape[0]
-    tile = mixed.shape[1] // count
+    tile = mixed.shape[0] // count
     writes = []
     for i in range(count):
-        columns = pl.ds(i * tile, tile)
-        mixed[:, columns] = jnp.dot(
-            combine[...], expert_out[:, columns], preferred_element_type=jnp.float32
+        rows = pl.ds(i * tile, tile)
+        mixed[rows, :] = jnp.dot(
+            combine[rows, :], expert_out[...], preferred_element_type=jnp.float32
         ).astype(mixed.dtype)
-        write = pltpu.make_async_copy(mixed.at[:, columns], out_hbm.at[0, :, columns], sems.at[i])
+        write = pltpu.make_async_copy(mixed.at[rows], out_hbm.at[0, rows], sems.at[i])
         write.start()
         writes.append(write)
     for write in writes:
@@ -330,7 +336,6 @@
             collective_id=0, has_side_effects=True, vmem_limit_bytes=60 * 1024 * 1024
         ),
     )(tokens, router, w_in, b_in, w_out, b_out)
-    tile = 2 * LANES
     return pl.pallas_call(
         mix_kernel,
         out_shape=jax.ShapeDtypeStruct(tokens.shape, bf16),
@@ -338,7 +343,7 @@
         out_specs=pl.BlockSpec(memory_space=pltpu.HBM),
         scratch_shapes=[
             pltpu.VMEM((m, width), bf16),
-            dma((width // tile,)),
+            dma((MIX_TILES,)),
         ],
         compiler_params=pltpu.CompilerParams(vmem_limit_bytes=8 * 1024 * 1024),
     )(combine, expert_out)

time: 41.1 us -> 41 us (level)
  no operation moved by 1% of the time
where the time goes in v5:
time: 41 us; the launch traced here: 40.9 us
  Pallas kernels  40.9 us (100%)
    pallas_call x1, Pallas kernels, shards(): pl.pallas_call(kernel, out_shape=[pltpu.VMEM((m, n_ex), bf16), pltpu.VMEM...  39.8 us
    pallas_call x1, Pallas kernels, shards(): pl.pallas_call(mix_kernel, out_shape=jax.ShapeDtypeStruct(tokens.shape, b...  1.07 us

profile of v5, /device:TPU:1, one launch (start us, length us, event | category | flops | bytes accessed | tf_op | source)
XLA Modules:
  0.0 40.9 jit_solution(1870217763551532136)
XLA Ops:
  0.0 39.8 %shard_map.64 = (bf16[256,128]{1,0:T(8,128)(2,1)S(1)}, bf16[128,1280]{1,0:T(8,128)(2,1)S(1)}) custom-call(bf16[1,256,1280]{2,1,0:T(8,128)(2,1)} %tokens_hbm.1, bf16[1280,128]{1,0:T(8,128)(2,1)} %router_hbm.1, bf16[1,1280,2560]{2,1,0:T(8,128)(2,1)} %w_in_hbm.1, bf16[1,5120]{1,0:T(2,128)(2,1)} %b_in_hbm.1, bf16[1,2560,1280]{2,1,0:T(8,128)(2,1)} %w_out_hbm.1, ...), custom_call_target="tpu_custom_call" | custom-call | tf_op jit(solution)/shard_map/pallas_call | solution.py:299
  39.8 1.1 %shard_map.65 = bf16[1,256,1280]{2,1,0:T(8,128)(2,1)} custom-call(bf16[256,128]{1,0:T(8,128)(2,1)S(1)} %get-tuple-element.7.combine, bf16[128,1280]{1,0:T(8,128)(2,1)S(1)} %get-tuple-element.8.expert_out), custom_call_target="tpu_custom_call" | custom-call | tf_op jit(solution)/shard_map/pallas_call | solution.py:339
